TPU v7x, 32 devices: a whole 2x2x4 slice. The times are simulated.
32 devices in a mesh: rep: 4 (over x, y), dp: 8 (over z, core).
Axes of the slice: x: 2, y: 2, z: 4, core: 2. Of those that a mesh axis runs over, the one named last changes fastest.
Arguments:
- g_w_gate: bfloat16 [32, 2, 1024, 3584], P(('rep', 'dp')), parts along dimension 0
- g_w_up: bfloat16 [32, 2, 1024, 3584], P(('rep', 'dp')), parts along dimension 0
- g_w_down: bfloat16 [32, 2, 3584, 1024], P(('rep', 'dp')), parts along dimension 0
- w_gate: bfloat16 [2, 1024, 3584], replicated
- w_up: bfloat16 [2, 1024, 3584], replicated
- w_down: bfloat16 [2, 3584, 1024], replicated
- m_w_gate: float32 [2, 1024, 3584], P(None, 'dp')
- m_w_up: float32 [2, 1024, 3584], P(None, 'dp')
- m_w_down: float32 [2, 3584, 1024], P(None, 'dp')
- v_w_gate: float32 [2, 1024, 3584], P(None, 'dp')
- v_w_up: float32 [2, 1024, 3584], P(None, 'dp')
- v_w_down: float32 [2, 3584, 1024], P(None, 'dp')
Outputs:
- output 1: bfloat16 [8, 1024, 3584], P('rep'), parts along dimension 0
- output 2: bfloat16 [8, 1024, 3584], P('rep'), parts along dimension 0
- output 3: bfloat16 [8, 3584, 1024], P('rep'), parts along dimension 0
- output 4: float32 [8, 1024, 3584], P('rep', 'dp'), parts along dimension 0
- output 5: float32 [8, 1024, 3584], P('rep', 'dp'), parts along dimension 0
- output 6: float32 [8, 3584, 1024], P('rep', 'dp'), parts along dimension 0
- output 7: float32 [8, 1024, 3584], P('rep', 'dp'), parts along dimension 0
- output 8: float32 [8, 1024, 3584], P('rep', 'dp'), parts along dimension 0
- output 9: float32 [8, 3584, 1024], P('rep', 'dp'), parts along dimension 0
There are 4 independent parts. A program takes and returns all parts, laid end to end along the dimension named above; an argument that names none is the same for every part.
All inputs are finite; a program needn't handle non-finite values.
Results may differ from a plain program's by a relative error of at most 0.022.
Values are sent between devices in bfloat16 or wider.
A program may use at most 2 GiB of HBM per device.

v0:
```python
import jax
import jax.numpy as jnp
from jax import lax
from jax.sharding import PartitionSpec as P


def adamw(w, m, v, g):
    m = 0.9 * m + 0.1 * g
    v = 0.95 * v + 0.05 * g * g
    step = m * lax.rsqrt(v + 1e-8) + 0.1 * w
    return (w - 0.02 * step).astype(jnp.bfloat16), m, v


def solution(mesh):
    def step(*arrays):
        terms, weights, m, v = (arrays[i : i + 3] for i in (0, 3, 6, 9))
        gradients = [lax.psum_scatter(t[0], "dp", scatter_dimension=1, tiled=True).astype(jnp.float32) for t in terms]
        me = lax.axis_index("dp")
        own = [lax.dynamic_slice_in_dim(w, me * one.shape[1], one.shape[1], 1).astype(jnp.float32) for w, one in zip(weights, m, strict=True)]
        new = [adamw(w, m, v, g) for w, m, v, g in zip(own, m, v, gradients, strict=True)]
        whole = [lax.all_gather(one[0], "dp", axis=1, tiled=True) for one in new]
        return (*whole, *(one[1] for one in new), *(one[2] for one in new))

    all_of, cut = P(None, None, None), P(None, "dp", None)
    return jax.shard_map(
        step,
        mesh=mesh,
        in_specs=(P(("rep", "dp"), None, None, None),) * 3 + (all_of,) * 3 + (cut,) * 6,
        out_specs=(P("rep", None, None),) * 3 + (P("rep", "dp", None),) * 6,
        check_vma=False,
    )
```

profile of v0, /device:TPU:0, one launch (start us, length us, event | category | flops | bytes accessed | tf_op | source)
XLA Modules:
  0.0 901.6 jit_solution(17996080168292664233)
XLA Ops:
  7.2 0.0 reduce-scatter.8.cloned.1.call-start
  7.2 0.7 reduce-scatter.8.cloned.1.call-update
  7.9 0.0 reduce-scatter.6.cloned.1.call-start
  8.0 0.7 reduce-scatter.6.cloned.1.call-update
  8.7 0.0 reduce-scatter.4.cloned.1.call-start
  8.7 0.7 reduce-scatter.4.cloned.1.call-update
  9.4 0.0 all-gather.8.cloned.1.call-start
  9.4 152.4 %reduce-scatter.8.cloned.1.call-done = bf16[2,448,1024]{2,1,0:T(8,128)(2,1)} async-done(((bf16[2,3584,1024]{2,1,0:T(8,128)(2,1)}), bf16[2,448,1024]{2,1,0:T(8,128)(2,1)}) %reduce-scatter.8.cloned.1.call-update) | async-done | bytes 1835024 | tf_op jit(solution)/shard_map/reduce_scatter | solution.py:17
  161.8 7.1 fusion.10
  168.9 0.0 all-gather.8.cloned.1.call-update
  168.9 0.0 all-gather.6.cloned.1.call-start
  169.0 142.6 %reduce-scatter.6.cloned.1.call-done = bf16[2,128,3584]{2,1,0:T(8,128)(2,1)} async-done(((bf16[2,1024,3584]{2,1,0:T(8,128)(2,1)}), bf16[2,128,3584]{2,1,0:T(8,128)(2,1)}) %reduce-scatter.6.cloned.1.call-update) | async-done | bytes 1835024 | tf_op jit(solution)/shard_map/reduce_scatter | solution.py:17
  311.6 7.2 fusion.6
  318.9 0.0 all-gather.6.cloned.1.call-update
  318.9 0.0 all-gather.4.cloned.1.call-start
  318.9 142.5 %reduce-scatter.4.cloned.1.call-done = bf16[2,128,3584]{2,1,0:T(8,128)(2,1)} async-done(((bf16[2,1024,3584]{2,1,0:T(8,128)(2,1)}), bf16[2,128,3584]{2,1,0:T(8,128)(2,1)}) %reduce-scatter.4.cloned.1.call-update) | async-done | bytes 1835024 | tf_op jit(solution)/shard_map/reduce_scatter | solution.py:17
  461.4 7.2 fusion.2
  468.7 0.0 all-gather.4.cloned.1.call-update
  468.7 127.1 %all-gather.8.cloned.1.call-done = bf16[2,3584,1024]{2,1,0:T(8,128)(2,1)} async-done(((bf16[2,448,1024]{2,1,0:T(8,128)(2,1)}), bf16[2,3584,1024]{2,1,0:T(8,128)(2,1)}) %all-gather.8.cloned.1.call-update) | async-done | bytes 14680080 | tf_op jit(solution)/shard_map/all_gather | solution.py:21
  595.8 134.5 %all-gather.6.cloned.1.call-done = bf16[2,1024,3584]{2,1,0:T(8,128)(2,1)} async-done(((bf16[2,128,3584]{2,1,0:T(8,128)(2,1)}), bf16[2,1024,3584]{2,1,0:T(8,128)(2,1)}) %all-gather.6.cloned.1.call-update) | async-done | bytes 14680080 | tf_op jit(solution)/shard_map/all_gather | solution.py:21
  730.2 134.5 %all-gather.4.cloned.1.call-done = bf16[2,1024,3584]{2,1,0:T(8,128)(2,1)} async-done(((bf16[2,128,3584]{2,1,0:T(8,128)(2,1)}), bf16[2,1024,3584]{2,1,0:T(8,128)(2,1)}) %all-gather.4.cloned.1.call-update) | async-done | bytes 14680080 | tf_op jit(solution)/shard_map/all_gather | solution.py:21
  864.7 0.0 copy-start
  864.7 0.0 slice-start
  864.7 0.0 slice-start.1
  864.7 0.0 slice-start.2
  864.7 15.7 %copy.24 = bf16[2,1024,3584]{2,1,0:T(8,128)(2,1)} copy(bf16[2,1024,3584]{2,1,0:T(8,128)(2,1)} %all-gather.4.cloned.1.call-done) | data formatting | bytes 29360128
  880.4 0.0 copy-done
  880.4 0.0 slice-start.3
  880.4 7.4 copy.25
  887.9 0.0 slice-done
  887.9 0.0 slice-done.1
  887.9 0.0 slice-done.2
  887.9 1.4 slice-done.3
  889.3 5.5 copy.26
  (1 shorter events, 0.0 us)
Async XLA Ops:
  7.2 154.7 %reduce-scatter.8.cloned.1.call-start = ((), (), s32[]{:S(2)}) async-start(), calls=%async_computation.7 | async-start | bytes 16515072 | tf_op jit(solution)/shard_map/reduce_scatter | solution.py:17
  7.9 303.7 %reduce-scatter.6.cloned.1.call-start = ((), (), s32[]{:S(2)}) async-start(), calls=%async_computation.5 | async-start | bytes 16515072 | tf_op jit(solution)/shard_map/reduce_scatter | solution.py:17
  8.7 452.7 %reduce-scatter.4.cloned.1.call-start = ((), (), s32[]{:S(2)}) async-start(), calls=%async_computation.3 | async-start | bytes 16515072 | tf_op jit(solution)/shard_map/reduce_scatter | solution.py:17
  9.4 586.4 %all-gather.8.cloned.1.call-start = ((), (), s32[]{:S(2)}) async-start(), calls=%async_computation.8 | async-start | bytes 16515072 | tf_op jit(solution)/shard_map/all_gather | solution.py:21
  168.9 561.3 %all-gather.6.cloned.1.call-start = ((), (), s32[]{:S(2)}) async-start(), calls=%async_computation.6 | async-start | bytes 16515072 | tf_op jit(solution)/shard_map/all_gather | solution.py:21
  318.9 545.8 %all-gather.4.cloned.1.call-start = ((), (), s32[]{:S(2)}) async-start(), calls=%async_computation.4 | async-start | bytes 16515072 | tf_op jit(solution)/shard_map/all_gather | solution.py:21
  864.7 15.7 %copy-start = (bf16[2,1024,3584]{2,1,0:T(8,128)(2,1)S(1)}, bf16[2,1024,3584]{2,1,0:T(8,128)(2,1)}, u32[]{:S(2)}) copy-start(bf16[2,1024,3584]{2,1,0:T(8,128)(2,1)} %all-gather.6.cloned.1.call-done) | copy-start | bytes 44040196
  864.7 23.2 %slice-start = ((s8[14680064]{0:T(1024)(128)(4,1)}), s8[4194304]{0:T(1024)(128)(4,1)S(1)}, s32[]{:S(2)}) async-start(s8[14680064]{0:T(1024)(128)(4,1)} %bitcast.6), calls=%async_computation.9 | async-start | bytes 8388608
  864.7 23.2 %slice-start.1 = ((s8[14680064]{0:T(1024)(128)(4,1)}), s8[4194304]{0:T(1024)(128)(4,1)S(1)}, s32[]{:S(2)}) async-start(s8[14680064]{0:T(1024)(128)(4,1)} %bitcast.6), calls=%async_computation.10 | async-start | bytes 8388608
  864.7 23.2 %slice-start.2 = ((s8[14680064]{0:T(1024)(128)(4,1)}), s8[4194304]{0:T(1024)(128)(4,1)S(1)}, s32[]{:S(2)}) async-start(s8[14680064]{0:T(1024)(128)(4,1)} %bitcast.6), calls=%async_computation.11 | async-start | bytes 8388608
  880.4 8.9 slice-start.3
Sparse Core Ops, SparseCore 0:
  10.3 151.4 reduce-scatter.7
  164.1 147.4 reduce-scatter.5
  313.9 147.4 reduce-scatter.3
  463.4 132.2 all-gather.7
  597.8 132.3 all-gather.5
  732.3 132.3 all-gather.3
where the time goes:
time: 902 us
  waiting for transfers between devices  836 us (93%)
  local copies, waits for them, and re-layouts  30.1 us (3%)
  other arithmetic  21.6 us (2%)
  between operations  14.1 us (2%)
    reduce_scatter x3, waiting for transfers between devices, step(): lax.psum_scatter(t[0], 'dp', scatter_dimension=1, tiled=True)  437 us
    all_gather x3, waiting for transfers between devices, step(): whole = [lax.all_gather(one[0], 'dp', axis=1, tiled=True) for one in new]  396 us
    unnamed x13, local copies, waits for them, and re-layouts  30.1 us
    convert_element_type x3, other arithmetic, adamw(): return ((w - 0.02 * step).astype(jnp.bfloat16), m, v)  21.6 us
  transfers between devices with their start and end apart: 6, of which 6 were waited for; matrix products, arithmetic and copies ran while one was open for 2% of the time, Pallas kernels for 0%

commit v1 on v0

v1 whole, which is shorter than its diff:
```python
import functools

import jax
import jax.numpy as jnp
from jax import lax
from jax.experimental import pallas as pl
from jax.experimental.pallas import tpu as pltpu
from jax.sharding import PartitionSpec as P

MESH = pl.DeviceIdType.MESH
N = 28
UNITS = 224
PER = UNITS // N
K = 6 * PER
H = 1
AHEAD = 2
EARLY = 2
LATE = 3
R = 8
CH = 7
SHAPES = ((1024, 3584), (1024, 3584), (3584, 1024))
F_OF = (3 * H, 2 * H, 2 * H, 3 * H)
STEPS = K + 6 * H + LATE + 1


def tiled(a, blocks):
    layers, rows, columns = a.shape
    a = a.reshape(layers, blocks, rows // blocks // 8, 8, columns // 128, 128).transpose(0, 1, 2, 4, 3, 5)
    return a.reshape(layers, blocks, -1, 16, 128)


def untiled(a, rows, columns):
    layers, blocks = a.shape[:2]
    a = a.reshape(layers, blocks, rows // blocks // 8, columns // 128, 8, 128).transpose(0, 1, 2, 4, 3, 5)
    return a.reshape(layers, rows, columns)


def kernel(*refs):
    g, w, m, v = refs[0:3], refs[3:6], refs[6:9], refs[9:12]
    W, MV = refs[12:14]
    own, part, inb, mvb = refs[14:18]
    own_sem, part_send, part_recv, rs_send, rs_recv, mv_load, mv_store, ag_send, ag_recv, p_send, p_recv = refs[18:]

    me = lax.axis_index("dp")
    z, c = me // 2, me % 2
    partner = me + 1 - 2 * c
    up, down = jnp.minimum(me + 2, 7), jnp.maximum(me - 2, 0)
    f_me = jnp.maximum(z, 3 - z) * H

    barrier = pltpu.get_barrier_semaphore()
    pl.semaphore_signal(barrier, inc=1, device_id={"dp": partner}, device_id_type=MESH)

    @pl.when(z < 3)
    def _():
        pl.semaphore_signal(barrier, inc=1, device_id={"dp": up}, device_id_type=MESH)

    @pl.when(z > 0)
    def _():
        pl.semaphore_signal(barrier, inc=1, device_id={"dp": down}, device_id_type=MESH)

    pl.semaphore_wait(barrier, jnp.where((z == 0) | (z == 3), 2, 3))

    def live(k):
        return (k >= 0) & (k < K)

    def place(k):
        return k // (2 * PER), (k // PER) % 2, pl.ds((k % PER) * N, N)

    def of_weight(k, do):
        for i in range(3):
            pl.when(k // (2 * PER) == i)(functools.partial(do, i))

    def remote(src, dst, send, recv, to):
        return pltpu.make_async_remote_copy(src_ref=src, dst_ref=dst, send_sem=send, recv_sem=recv, device_id={"dp": to}, device_id_type=MESH)

    def wait_unit(sem):
        pltpu.make_async_copy(inb.at[0, 0], inb.at[0, 0], sem).wait()

    def wait_own(sem):
        pltpu.make_async_copy(own.at[0], own.at[0], sem).wait()

    def wait_moment(sem):
        pltpu.make_async_copy(mvb.at[0, 0], mvb.at[0, 0], sem).wait()

    def add(slot, zp, more):
        def chunk(i, _):
            at = pl.ds(i * CH, CH)
            s = own[slot, zp, at].astype(jnp.float32) + part[slot, zp, at].astype(jnp.float32)
            for idx in more:
                s = s + inb[slot, idx, at].astype(jnp.float32)
            own[slot, zp, at] = s.astype(jnp.bfloat16)
            return 0

        lax.fori_loop(0, N // CH, chunk, 0)

    def step_on(slot, k, more):
        wt, layer, _ = place(k)
        base = (k % PER) * N

        def chunk(i, _):
            at = pl.ds(i * CH, CH)
            s = own[slot, z, at].astype(jnp.float32) + part[slot, z, at].astype(jnp.float32)
            for idx in more:
                s = s + inb[slot, idx, at].astype(jnp.float32)
            grad = s.astype(jnp.bfloat16).astype(jnp.float32)
            here = pl.ds(base + i * CH, CH)
            weight = W[wt, layer, me, here].astype(jnp.float32)
            mom = 0.9 * mvb[slot, 0, at] + 0.1 * grad
            var = 0.95 * mvb[slot, 1, at] + 0.05 * grad * grad
            mvb[slot, 0, at] = mom
            mvb[slot, 1, at] = var
            W[wt, layer, me, here] = (weight - 0.02 * (mom * lax.rsqrt(var + 1e-8) + 0.1 * weight)).astype(jnp.bfloat16)
            return 0

        lax.fori_loop(0, N // CH, chunk, 0)

    def block(k, zp, cc):
        wt, layer, at = place(k)
        return W.at[wt, layer, 2 * zp + cc, at]

    def body(t, _):
        t = t - AHEAD

        for zp in range(4):
            k = t - LATE - jnp.where(zp > z, z, 3 - z) * H

            @pl.when(live(k) & (zp != z))
            def _(k=k, zp=zp):
                wait_unit(rs_send.at[k % R, zp])

        @pl.when(live(t))
        def _():
            wait_own(own_sem.at[t % R])
            wait_own(part_recv.at[t % R])
            wait_own(part_send.at[t % R])

        ka = t + AHEAD

        @pl.when(live(ka))
        def _():
            slot = ka % R
            _, layer, at = place(ka)

            def do(i):
                pltpu.make_async_copy(g[i].at[layer, :, c, at], own.at[slot], own_sem.at[slot]).start()
                remote(g[i].at[layer, :, 1 - c, at], part.at[slot], part_send.at[slot], part_recv.at[slot], partner).start()

            of_weight(ka, do)

        ks = t - f_me - LATE

        @pl.when(live(ks))
        def _():
            wait_moment(mv_store.at[ks % R, 0])
            wait_moment(mv_store.at[ks % R, 1])

        km = t - f_me + EARLY

        @pl.when(live(km))
        def _():
            slot = km % R
            _, layer, at = place(km)

            def do(i):
                pltpu.make_async_copy(m[i].at[layer, 0, at], mvb.at[slot, 0], mv_load.at[slot, 0]).start()
                pltpu.make_async_copy(v[i].at[layer, 0, at], mvb.at[slot, 1], mv_load.at[slot, 1]).start()
                pltpu.make_async_copy(w[i].at[layer, me, at], W.at[i, layer, me, at], mv_load.at[slot, 2]).start()

            of_weight(km, do)

        ku, kd = t - z * H, t - (3 - z) * H
        for far in range(3):
            zp = 3 - far

            @pl.when(live(ku) & (zp > z))
            def _(zp=zp):
                slot = ku % R

                @pl.when(z == 0)
                def _():
                    add(slot, zp, ())

                @pl.when(z > 0)
                def _():
                    wait_unit(rs_recv.at[slot, zp])
                    add(slot, zp, (zp,))

                remote(own.at[slot, zp], inb.at[slot, zp], rs_send.at[slot, zp], rs_recv.at[slot, zp], up).start()

            zq = far

            @pl.when(live(kd) & (zq < z))
            def _(zq=zq):
                slot = kd % R

                @pl.when(z == 3)
                def _():
                    add(slot, zq, ())

                @pl.when(z < 3)
                def _():
                    wait_unit(rs_recv.at[slot, zq])
                    add(slot, zq, (zq,))

                idx = jnp.where(zq == z - 1, 4, zq)
                remote(own.at[slot, zq], inb.at[slot, idx], rs_send.at[slot, zq], rs_recv.at[slot, idx], down).start()

        kf = t - f_me

        @pl.when(live(kf))
        def _():
            slot = kf % R
            wait_moment(mv_load.at[slot, 0])
            wait_moment(mv_load.at[slot, 1])
            wait_unit(mv_load.at[slot, 2])

            @pl.when(z > 0)
            def _():
                wait_unit(rs_recv.at[slot, z])

            @pl.when(z < 3)
            def _():
                wait_unit(rs_recv.at[slot, 4])

            @pl.when(z == 0)
            def _():
                step_on(slot, kf, (4,))

            @pl.when(z == 3)
            def _():
                step_on(slot, kf, (3,))

            @pl.when((z > 0) & (z < 3))
            def _():
                step_on(slot, kf, (z, 4))

            mine = block(kf, z, c)

            @pl.when(z < 3)
            def _():
                remote(mine, mine, ag_send.at[slot, z], ag_recv.at[slot, z], up).start()

            @pl.when(z > 0)
            def _():
                remote(mine, mine, ag_send.at[slot, 4], ag_recv.at[slot, z], down).start()

            remote(mine, mine, p_send.at[slot, z], p_recv.at[slot, z], partner).start()
            wt, layer, at = place(kf)
            pltpu.make_async_copy(mvb.at[slot, 0], MV.at[0, wt, layer, at], mv_store.at[slot, 0]).start()
            pltpu.make_async_copy(mvb.at[slot, 1], MV.at[1, wt, layer, at], mv_store.at[slot, 1]).start()

        for near in range(3):
            zp = 2 - near
            kb = t - F_OF[zp] - (z - zp) * H

            @pl.when(live(kb) & (zp < z))
            def _(zp=zp, k=kb):
                slot = k % R
                wait_unit(ag_recv.at[slot, zp])
                there = block(k, zp, c)

                @pl.when(z < 3)
                def _():
                    remote(there, there, ag_send.at[slot, zp], ag_recv.at[slot, zp], up).start()

                remote(there, there, p_send.at[slot, zp], p_recv.at[slot, zp], partner).start()

            zq = 1 + near
            kc = t - F_OF[zq] - (zq - z) * H

            @pl.when(live(kc) & (zq > z))
            def _(zq=zq, k=kc):
                slot = k % R
                wait_unit(ag_recv.at[slot, zq])
                there = block(k, zq, c)

                @pl.when(z > 0)
                def _():
                    remote(there, there, ag_send.at[slot, zq], ag_recv.at[slot, zq], down).start()

                remote(there, there, p_send.at[slot, zq], p_recv.at[slot, zq], partner).start()

        for zp in range(4):
            ksent = t - F_OF[zp] - jnp.abs(z - zp) * H

            @pl.when(live(ksent - 1))
            def _(zp=zp, k=ksent - 1):
                wait_unit(p_recv.at[k % R, zp])

            @pl.when(live(ksent - LATE))
            def _(zp=zp, k=ksent - LATE):
                wait_unit(p_send.at[k % R, zp])

                @pl.when((zp < z) & (z < 3))
                def _():
                    wait_unit(ag_send.at[k % R, zp])

                @pl.when((zp > z) & (z > 0))
                def _():
                    wait_unit(ag_send.at[k % R, zp])

                @pl.when((zp == z) & (z < 3))
                def _():
                    wait_unit(ag_send.at[k % R, zp])

                @pl.when((zp == z) & (z > 0))
                def _():
                    wait_unit(ag_send.at[k % R, 4])

        return 0

    lax.fori_loop(0, STEPS + AHEAD, body, 0)


def solution(mesh):
    def step(*arrays):
        g = [tiled(a[0], 8).reshape(2, 4, 2, UNITS, 16, 128) for a in arrays[:3]]
        w = [tiled(a, 8) for a in arrays[3:6]]
        moments = [tiled(a, 1) for a in arrays[6:]]
        hbm = pl.BlockSpec(memory_space=pl.ANY)
        piece = (N, 16, 128)
        dma = pltpu.SemaphoreType.DMA
        new, mv = pl.pallas_call(
            kernel,
            out_shape=[
                jax.ShapeDtypeStruct((3, 2, 8, UNITS, 16, 128), jnp.bfloat16),
                jax.ShapeDtypeStruct((2, 3, 2, UNITS, 16, 128), jnp.float32),
            ],
            in_specs=[hbm] * 12,
            out_specs=[hbm, hbm] if False else [pl.BlockSpec(memory_space=pltpu.VMEM), hbm],
            scratch_shapes=[
                pltpu.VMEM((R, 4, *piece), jnp.bfloat16),
                pltpu.VMEM((R, 4, *piece), jnp.bfloat16),
                pltpu.VMEM((R, 5, *piece), jnp.bfloat16),
                pltpu.VMEM((R, 2, *piece), jnp.float32),
                dma((R,)),
                dma((R,)),
                dma((R,)),
                dma((R, 4)),
                dma((R, 5)),
                dma((R, 3)),
                dma((R, 2)),
                dma((R, 5)),
                dma((R, 4)),
                dma((R, 4)),
                dma((R, 4)),
            ],
            compiler_params=pltpu.CompilerParams(collective_id=0, has_side_effects=True, vmem_limit_bytes=62 * 1024 * 1024),
            name="sum_step_spread",
        )(*g, *w, *moments)
        whole = [untiled(new[i], *SHAPES[i]) for i in range(3)]
        rest = [untiled(mv[which, i][:, None], SHAPES[i][0] // 8, SHAPES[i][1]) for which in range(2) for i in range(3)]
        return (*whole, *rest)

    all_of, cut = P(None, None, None), P(None, "dp", None)
    return jax.shard_map(
        step,
        mesh=mesh,
        in_specs=(P(("rep", "dp"), None, None, None),) * 3 + (all_of,) * 3 + (cut,) * 6,
        out_specs=(P("rep", None, None),) * 3 + (P("rep", "dp", None),) * 6,
        check_vma=False,
    )
```

time: 902 us -> 565 us (0.63)
  waiting for transfers between devices: 836 us -> 0 us
  Pallas kernels: 0 us -> 514 us
  other arithmetic: 21.6 us -> 0 us
  local copies, waits for them, and re-layouts: 30.1 us -> 50.1 us
  between operations: 14.1 us -> 0.66 us
    pallas_call x0 -> x1, Pallas kernels: none -> 514 us  [step(): pl.pallas_call(kernel, out_shape=[jax.ShapeDtypeStruct((3, 2, 8, UNITS, 1...]
    reduce_scatter x3 -> x0, waiting for transfers between devices: 437 us -> none  [step(): lax.psum_scatter(t[0], 'dp', scatter_dimension=1, tiled=True)]
    all_gather x3 -> x0, waiting for transfers between devices: 396 us -> none  [step(): whole = [lax.all_gather(one[0], 'dp', axis=1, tiled=True) for one in new]]
    slice x0 -> x2, local copies, waits for them, and re-layouts: none -> 50.1 us  [the longest x1 34.7 us: step(): whole = [untiled(new[i], *SHAPES[i]) for i in range(3)]]
    unnamed x13 -> x0, local copies, waits for them, and re-layouts: 30.1 us -> none
    convert_element_type x3 -> x0, other arithmetic: 21.6 us -> none  [adamw(): return ((w - 0.02 * step).astype(jnp.bfloat16), m, v)]
  transfers between devices with their start and end apart: 6 -> 0, of which waited for: 6 -> 0; matrix products, arithmetic and copies ran while one was open for 2% -> 0% of each run, Pallas kernels for 0% -> 0%
where the time goes in v1:
time: 565 us
  Pallas kernels  514 us (91%)
  local copies, waits for them, and re-layouts  50.1 us (9%)
    pallas_call x1, Pallas kernels, step(): pl.pallas_call(kernel, out_shape=[jax.ShapeDtypeStruct((3, 2, 8, UNITS, 1...  514 us
    slice x1, local copies, waits for them, and re-layouts, step(): whole = [untiled(new[i], *SHAPES[i]) for i in range(3)]  34.7 us
    slice x1, local copies, waits for them, and re-layouts, step(): mv[which, i][:, None]  15.4 us

profile of v1, /device:TPU:0, one launch (start us, length us, event | category | flops | bytes accessed | tf_op | source)
XLA Modules:
  0.0 564.6 jit_solution(17981250256413300451)
XLA Ops:
  0.6 513.8 %sum_step_spread.1 = (bf16[3,2,8,224,16,128]{5,4,3,2,1,0:T(8,128)(2,1)}, f32[2,3,2,224,16,128]{5,4,3,2,1,0:T(8,128)}) custom-call(bf16[2,4,2,224,16,128]{5,4,3,2,1,0:T(8,128)(2,1)} %bitcast.105, bf16[2,4,2,224,16,128]{5,4,3,2,1,0:T(8,128)(2,1)} %bitcast.106, bf16[2,4,2,224,16,128]{5,4,3,2,1,0:T(8,128)(2,1)} %bitcast.107, ...), custom_call_target="tpu_custom_call" | custom-call | tf_op jit(solution)/shard_map/sum_step_spread/pallas_call | solution.py:323
  514.5 34.7 %fusion = (bf16[1,2,8,224,16,128]{5,4,3,2,1,0:T(8,128)(2,1)}, bf16[1,2,8,224,16,128]{5,4,3,2,1,0:T(8,128)(2,1)}, bf16[1,2,8,224,16,128]{5,4,3,2,1,0:T(8,128)(2,1)}) fusion(bf16[3,2,8,224,16,128]{5,4,3,2,1,0:T(8,128)(2,1)} %get-tuple-element.11), kind=kLoop, calls=%fused_computation | loop fusion | bytes 88080384 | tf_op jit(solution)/shard_map/slice | solution.py:351
  549.1 15.4 %fusion.1 = (f32[1,1,2,224,16,128]{5,4,3,2,1,0:T(8,128)}, f32[1,1,2,224,16,128]{5,4,3,2,1,0:T(8,128)}, f32[1,1,2,224,16,128]{5,4,3,2,1,0:T(8,128)}, f32[1,1,2,22...) fusion(f32[2,3,2,224,16,128]{5,4,3,2,1,0:T(8,128)} %get-tuple-element.12), kind=kLoop, calls=%fused_computation.1 | loop fusion | bytes 44040192 | tf_op jit(solution)/shard_map/slice | solution.py:352

commit v2 on v1

--- a/solution.py
+++ b/solution.py
@@ -8,7 +8,7 @@
 from jax.sharding import PartitionSpec as P
 
 MESH = pl.DeviceIdType.MESH
-N = 28
+N = 14
 UNITS = 224
 PER = UNITS // N
 K = 6 * PER
@@ -18,6 +18,8 @@
 LATE = 3
 R = 8
 CH = 7
+NV = 2
+LIMIT = 7.75
 SHAPES = ((1024, 3584), (1024, 3584), (3584, 1024))
 F_OF = (3 * H, 2 * H, 2 * H, 3 * H)
 STEPS = K + 6 * H + LATE + 1
@@ -37,9 +39,9 @@
 
 def kernel(*refs):
     g, w, m, v = refs[0:3], refs[3:6], refs[6:9], refs[9:12]
-    W, MV = refs[12:14]
-    own, part, inb, mvb = refs[14:18]
-    own_sem, part_send, part_recv, rs_send, rs_recv, mv_load, mv_store, ag_send, ag_recv, p_send, p_recv = refs[18:]
+    W, MVV, MV = refs[12:15]
+    own, part, inb, mvb = refs[15:19]
+    own_sem, part_send, part_recv, rs_send, rs_recv, mv_load, mv_store, ag_send, ag_recv, p_send, p_recv = refs[19:]
 
     me = lax.axis_index("dp")
     z, c = me // 2, me % 2
@@ -246,8 +248,16 @@
 
             remote(mine, mine, p_send.at[slot, z], p_recv.at[slot, z], partner).start()
             wt, layer, at = place(kf)
-            pltpu.make_async_copy(mvb.at[slot, 0], MV.at[0, wt, layer, at], mv_store.at[slot, 0]).start()
-            pltpu.make_async_copy(mvb.at[slot, 1], MV.at[1, wt, layer, at], mv_store.at[slot, 1]).start()
+
+            @pl.when(wt < NV)
+            def _():
+                for which in range(2):
+                    pltpu.make_async_copy(mvb.at[slot, which], MVV.at[which, wt, layer, at], mv_store.at[slot, which]).start()
+
+            @pl.when(wt >= NV)
+            def _():
+                for which in range(2):
+                    pltpu.make_async_copy(mvb.at[slot, which], MV.at[which, wt - NV, layer, at], mv_store.at[slot, which]).start()
 
         for near in range(3):
             zp = 2 - near
@@ -312,22 +322,45 @@
     lax.fori_loop(0, STEPS + AHEAD, body, 0)
 
 
+def put_out(*refs):
+    W, MVV, MV = refs[0:3]
+    whole, rest = refs[3:6], refs[6:12]
+    held, load, store, keep = refs[12:16]
+    parts = [(which, i, layer) for i in range(NV, 3) for which in range(2) for layer in range(2)]
+    for j, (which, i, layer) in enumerate(parts):
+        pltpu.make_async_copy(MV.at[which, i - NV, layer], held.at[j], load.at[j]).start()
+    copies = [pltpu.make_async_copy(W.at[i], whole[i], keep.at[i]) for i in range(3)]
+    for i in range(NV):
+        for which in range(2):
+            copies.append(pltpu.make_async_copy(MVV.at[which, i], rest[3 * which + i].at[:, 0], keep.at[3 + 2 * i + which]))
+    for copy in copies:
+        copy.start()
+    for j, (which, i, layer) in enumerate(parts):
+        pltpu.make_async_copy(MV.at[which, i - NV, layer], held.at[j], load.at[j]).wait()
+        copy = pltpu.make_async_copy(held.at[j], rest[3 * which + i].at[layer, 0], store.at[j])
+        copy.start()
+        copies.append(copy)
+    for copy in copies:
+        copy.wait()
+
+
 def solution(mesh):
     def step(*arrays):
         g = [tiled(a[0], 8).reshape(2, 4, 2, UNITS, 16, 128) for a in arrays[:3]]
         w = [tiled(a, 8) for a in arrays[3:6]]
         moments = [tiled(a, 1) for a in arrays[6:]]
-        hbm = pl.BlockSpec(memory_space=pl.ANY)
+        hbm, vmem = pl.BlockSpec(memory_space=pl.ANY), pl.BlockSpec(memory_space=pltpu.VMEM)
         piece = (N, 16, 128)
         dma = pltpu.SemaphoreType.DMA
-        new, mv = pl.pallas_call(
+        new, kept, mv = pl.pallas_call(
             kernel,
             out_shape=[
-                jax.ShapeDtypeStruct((3, 2, 8, UNITS, 16, 128), jnp.bfloat16),
-                jax.ShapeDtypeStruct((2, 3, 2, UNITS, 16, 128), jnp.float32),
+                pltpu.VMEM((3, 2, 8, UNITS, 16, 128), jnp.bfloat16),
+                pltpu.VMEM((2, NV, 2, UNITS, 16, 128), jnp.float32),
+                jax.ShapeDtypeStruct((2, 3 - NV, 2, UNITS, 16, 128), jnp.float32),
             ],
             in_specs=[hbm] * 12,
-            out_specs=[hbm, hbm] if False else [pl.BlockSpec(memory_space=pltpu.VMEM), hbm],
+            out_specs=[vmem, vmem, hbm],
             scratch_shapes=[
                 pltpu.VMEM((R, 4, *piece), jnp.bfloat16),
                 pltpu.VMEM((R, 4, *piece), jnp.bfloat16),
@@ -345,11 +378,21 @@
                 dma((R, 4)),
                 dma((R, 4)),
             ],
-            compiler_params=pltpu.CompilerParams(collective_id=0, has_side_effects=True, vmem_limit_bytes=62 * 1024 * 1024),
+            compiler_params=pltpu.CompilerParams(collective_id=0, has_side_effects=True, vmem_limit_bytes=int(LIMIT * 2**20)),
             name="sum_step_spread",
         )(*g, *w, *moments)
-        whole = [untiled(new[i], *SHAPES[i]) for i in range(3)]
-        rest = [untiled(mv[which, i][:, None], SHAPES[i][0] // 8, SHAPES[i][1]) for which in range(2) for i in range(3)]
+        parts = 4 * (3 - NV)
+        outs = pl.pallas_call(
+            put_out,
+            out_shape=[jax.ShapeDtypeStruct((2, 8, UNITS, 16, 128), jnp.bfloat16)] * 3 + [jax.ShapeDtypeStruct((2, 1, UNITS, 16, 128), jnp.float32)] * 6,
+            in_specs=[vmem, vmem, hbm],
+            out_specs=[hbm] * 9,
+            scratch_shapes=[pltpu.VMEM((parts, UNITS, 16, 128), jnp.float32), dma((parts,)), dma((parts,)), dma((3 + 2 * NV,))],
+            compiler_params=pltpu.CompilerParams(vmem_limit_bytes=int(LIMIT * 2**20)),
+            name="put_out",
+        )(*(pltpu.with_memory_space_constraint(x, pltpu.VMEM) for x in (new, kept)), pltpu.with_memory_space_constraint(mv, pltpu.HBM))
+        whole = [untiled(outs[i], *SHAPES[i]) for i in range(3)]
+        rest = [untiled(outs[3 + i], SHAPES[i % 3][0] // 8, SHAPES[i % 3][1]) for i in range(6)]
         return (*whole, *rest)
 
     all_of, cut = P(None, None, None), P(None, "dp", None)

time: 565 us -> 518 us (0.917)
  local copies, waits for them, and re-layouts: 50.1 us -> 0 us
    slice x2 -> x0, local copies, waits for them, and re-layouts: 50.1 us -> none  [the longest x1 34.7 us: step(): whole = [untiled(new[i], *SHAPES[i]) for i in range(3)]]
    pallas_call x1 -> x2, Pallas kernels: 514 us -> 517 us  [the longest x1 494 us: step(): pl.pallas_call(kernel, out_shape=[pltpu.VMEM((3, 2, 8, UNITS, 16, 128), j...]
where the time goes in v2:
time: 518 us
  Pallas kernels  517 us (100%)
    pallas_call x1, Pallas kernels, step(): pl.pallas_call(kernel, out_shape=[pltpu.VMEM((3, 2, 8, UNITS, 16, 128), j...  494 us
    pallas_call x1, Pallas kernels, step(): pl.pallas_call(put_out, out_shape=[jax.ShapeDtypeStruct((2, 8, UNITS, 16,...  23.1 us

profile of v2, /device:TPU:0, one launch (start us, length us, event | category | flops | bytes accessed | tf_op | source)
XLA Modules:
  0.0 517.9 jit_solution(14947754644253750951)
XLA Ops:
  0.6 494.2 %sum_step_spread.1 = (bf16[3,2,8,224,16,128]{5,4,3,2,1,0:T(8,128)(2,1)S(1)}, f32[2,2,2,224,16,128]{5,4,3,2,1,0:T(8,128)S(1)}, f32[2,1,2,224,16,128]{5,4,3,2,1,0:T(8,128)}) custom-call(bf16[2,4,2,224,16,128]{5,4,3,2,1,0:T(8,128)(2,1)} %bitcast.105, bf16[2,4,2,224,16,128]{5,4,3,2,1,0:T(8,128)(2,1)} %bitcast.106, bf16[2,4,2,224,16,128]{5,4,3,2,1,0:T(8,128)(2,1)} %bitcast.107, ...), custom_call_target="tpu_custom_call" | custom-call | tf_op jit(solution)/shard_map/sum_step_spread/pallas_call | solution.py:355
  494.9 23.1 %put_out.1 = (bf16[2,8,224,16,128]{4,3,2,1,0:T(8,128)(2,1)}, bf16[2,8,224,16,128]{4,3,2,1,0:T(8,128)(2,1)}, bf16[2,8,224,16,128]{4,3,2,1,0:T(8,128)(2,1)}, f32[2...) custom-call(bf16[3,2,8,224,16,128]{5,4,3,2,1,0:T(8,128)(2,1)S(1)} %g, ...), custom_call_target="tpu_custom_call" | custom-call | tf_op jit(solution)/shard_map/put_out/pallas_call | solution.py:385

commit v3 on v2

v3 whole, which is shorter than its diff:
```python
import functools

import jax
import jax.numpy as jnp
from jax import lax
from jax.experimental import pallas as pl
from jax.experimental.pallas import tpu as pltpu
from jax.sharding import PartitionSpec as P

MESH = pl.DeviceIdType.MESH
N = 14
UNITS = 224
PER = UNITS // N
K = 6 * PER
H = 1
AHEAD = 1
EARLY = 2
LATE = 3
R = 8
R2 = 6
S = 2
G = 1
ORDER = (0, 1, 2)
CH = 7
NV = 2
LIMIT = 7.75
SHAPES = ((1024, 3584), (1024, 3584), (3584, 1024))
F_OF = (3 * H, 2 * H + S, 2 * H + S, 3 * H)
LAG = (0, S, S, 0)
STEPS = K + max(3 * H + 3 * G, 2 * H + S + 2 * G) + LATE + 1


def tiled(a, blocks):
    layers, rows, columns = a.shape
    a = a.reshape(layers, blocks, rows // blocks // 8, 8, columns // 128, 128).transpose(0, 1, 2, 4, 3, 5)
    return a.reshape(layers, blocks, -1, 16, 128)


def untiled(a, rows, columns):
    layers, blocks = a.shape[:2]
    a = a.reshape(layers, blocks, rows // blocks // 8, columns // 128, 8, 128).transpose(0, 1, 2, 4, 3, 5)
    return a.reshape(layers, rows, columns)


def kernel(*refs):
    g, w, m, v = refs[0:3], refs[3:6], refs[6:9], refs[9:12]
    W, MVV, MV = refs[12:15]
    own, part, inb, mvb = refs[15:19]
    own_sem, part_send, part_recv, rs_send, rs_recv, mv_load, mv_store, ag_send, ag_recv, p_send, p_recv = refs[19:]

    me = lax.axis_index("dp")
    z, c = me // 2, me % 2
    partner = me + 1 - 2 * c
    up, down = jnp.minimum(me + 2, 7), jnp.maximum(me - 2, 0)
    f_me = jnp.where((z == 0) | (z == 3), F_OF[0], F_OF[1])

    def live(k):
        return (k >= 0) & (k < K)

    def place(k):
        return k // (2 * PER), (k // PER) % 2, pl.ds((k % PER) * N, N)

    def of_weight(k, do):
        for i in range(3):
            pl.when(k // (2 * PER) == i)(functools.partial(do, i))

    def remote(src, dst, send, recv, to):
        return pltpu.make_async_remote_copy(src_ref=src, dst_ref=dst, send_sem=send, recv_sem=recv, device_id={"dp": to}, device_id_type=MESH)

    def wait_unit(sem):
        pltpu.make_async_copy(inb.at[0, 0], inb.at[0, 0], sem).wait()

    def wait_own(sem):
        pltpu.make_async_copy(own.at[0], own.at[0], sem).wait()

    def wait_moment(sem):
        pltpu.make_async_copy(mvb.at[0, 0], mvb.at[0, 0], sem).wait()

    def load_own(k):
        slot = k % R
        _, layer, at = place(k)
        of_weight(k, lambda i: pltpu.make_async_copy(g[i].at[layer, :, c, at], own.at[slot], own_sem.at[slot]).start())

    def send_part(k):
        slot = k % R
        _, layer, at = place(k)
        of_weight(k, lambda i: remote(g[i].at[layer, :, 1 - c, at], part.at[slot], part_send.at[slot], part_recv.at[slot], partner).start())

    def load_moments(k):
        slot = k % R2
        _, layer, at = place(k)

        def do(i):
            pltpu.make_async_copy(m[i].at[layer, 0, at], mvb.at[slot, 0], mv_load.at[slot, 0]).start()
            pltpu.make_async_copy(v[i].at[layer, 0, at], mvb.at[slot, 1], mv_load.at[slot, 1]).start()
            pltpu.make_async_copy(w[i].at[layer, me, at], W.at[i, layer, me, at], mv_load.at[slot, 2]).start()

        of_weight(k, do)

    barrier = pltpu.get_barrier_semaphore()
    pl.semaphore_signal(barrier, inc=1, device_id={"dp": partner}, device_id_type=MESH)

    @pl.when(z < 3)
    def _():
        pl.semaphore_signal(barrier, inc=1, device_id={"dp": up}, device_id_type=MESH)

    @pl.when(z > 0)
    def _():
        pl.semaphore_signal(barrier, inc=1, device_id={"dp": down}, device_id_type=MESH)

    for k in range(AHEAD):
        load_own(k)

    pl.semaphore_wait(barrier, jnp.where((z == 0) | (z == 3), 2, 3))

    for k in range(AHEAD):
        send_part(k)

    def add(slot, zp, more):
        def chunk(i, _):
            at = pl.ds(i * CH, CH)
            s = own[slot, zp, at].astype(jnp.float32) + part[slot, zp, at].astype(jnp.float32)
            for idx in more:
                s = s + inb[slot, idx, at].astype(jnp.float32)
            own[slot, zp, at] = s.astype(jnp.bfloat16)
            return 0

        lax.fori_loop(0, N // CH, chunk, 0)

    def step_on(slot, ms, k, more):
        wt, layer, _ = place(k)
        base = (k % PER) * N

        def chunk(i, _):
            at = pl.ds(i * CH, CH)
            s = own[slot, z, at].astype(jnp.float32) + part[slot, z, at].astype(jnp.float32)
            for idx in more:
                s = s + inb[slot, idx, at].astype(jnp.float32)
            grad = s.astype(jnp.bfloat16).astype(jnp.float32)
            here = pl.ds(base + i * CH, CH)
            weight = W[wt, layer, me, here].astype(jnp.float32)
            mom = 0.9 * mvb[ms, 0, at] + 0.1 * grad
            var = 0.95 * mvb[ms, 1, at] + 0.05 * grad * grad
            mvb[ms, 0, at] = mom
            mvb[ms, 1, at] = var
            W[wt, layer, me, here] = (weight - 0.02 * (mom * lax.rsqrt(var + 1e-8) + 0.1 * weight)).astype(jnp.bfloat16)
            return 0

        lax.fori_loop(0, N // CH, chunk, 0)

    def block(k, zp, cc):
        wt, layer, at = place(k)
        return W.at[wt, layer, 2 * zp + cc, at]

    def body(t, _):
        for zp in range(4):
            k = t - LATE - jnp.where(zp > z, z, 3 - z) * H - LAG[zp]

            @pl.when(live(k) & (zp != z))
            def _(k=k, zp=zp):
                wait_unit(rs_send.at[k % R, zp])

        @pl.when(live(t))
        def _():
            wait_own(own_sem.at[t % R])
            wait_own(part_recv.at[t % R])
            wait_own(part_send.at[t % R])

        ka = t + AHEAD

        @pl.when(live(ka))
        def _():
            load_own(ka)
            send_part(ka)

        ks = t - f_me - LATE

        @pl.when(live(ks))
        def _():
            wait_moment(mv_store.at[ks % R2, 0])
            wait_moment(mv_store.at[ks % R2, 1])

        km = t - f_me + EARLY

        @pl.when(live(km))
        def _():
            load_moments(km)

        def sums():
            for far in range(3):
                zp = 3 - far
                ku = t - z * H - LAG[zp]

                @pl.when(live(ku) & (zp > z))
                def _(zp=zp, ku=ku):
                    slot = ku % R

                    @pl.when(z == 0)
                    def _():
                        add(slot, zp, ())

                    @pl.when(z > 0)
                    def _():
                        wait_unit(rs_recv.at[slot, zp])
                        add(slot, zp, (zp,))

                    remote(own.at[slot, zp], inb.at[slot, zp], rs_send.at[slot, zp], rs_recv.at[slot, zp], up).start()

                zq = far
                kd = t - (3 - z) * H - LAG[zq]

                @pl.when(live(kd) & (zq < z))
                def _(zq=zq, kd=kd):
                    slot = kd % R

                    @pl.when(z == 3)
                    def _():
                        add(slot, zq, ())

                    @pl.when(z < 3)
                    def _():
                        wait_unit(rs_recv.at[slot, zq])
                        add(slot, zq, (zq,))

                    idx = jnp.where(zq == z - 1, 4, zq)
                    remote(own.at[slot, zq], inb.at[slot, idx], rs_send.at[slot, zq], rs_recv.at[slot, idx], down).start()

        def take_step():
            kf = t - f_me

            @pl.when(live(kf))
            def _():
                slot, ms = kf % R, kf % R2
                wait_moment(mv_load.at[ms, 0])
                wait_moment(mv_load.at[ms, 1])
                wait_unit(mv_load.at[ms, 2])

                @pl.when(z > 0)
                def _():
                    wait_unit(rs_recv.at[slot, z])

                @pl.when(z < 3)
                def _():
                    wait_unit(rs_recv.at[slot, 4])

                @pl.when(z == 0)
                def _():
                    step_on(slot, ms, kf, (4,))

                @pl.when(z == 3)
                def _():
                    step_on(slot, ms, kf, (3,))

                @pl.when((z > 0) & (z < 3))
                def _():
                    step_on(slot, ms, kf, (z, 4))

                mine = block(kf, z, c)

                @pl.when(z < 3)
                def _():
                    remote(mine, mine, ag_send.at[slot, z], ag_recv.at[slot, z], up).start()

                @pl.when(z > 0)
                def _():
                    remote(mine, mine, ag_send.at[slot, 4], ag_recv.at[slot, z], down).start()

                remote(mine, mine, p_send.at[slot, z], p_recv.at[slot, z], partner).start()
                wt, layer, at = place(kf)

                @pl.when(wt < NV)
                def _():
                    for which in range(2):
                        pltpu.make_async_copy(mvb.at[ms, which], MVV.at[which, wt, layer, at], mv_store.at[ms, which]).start()

                @pl.when(wt >= NV)
                def _():
                    for which in range(2):
                        pltpu.make_async_copy(mvb.at[ms, which], MV.at[which, wt - NV, layer, at], mv_store.at[ms, which]).start()

        def spread():
            for near in range(3):
                zp = 2 - near
                kb = t - F_OF[zp] - (z - zp) * G

                @pl.when(live(kb) & (zp < z))
                def _(zp=zp, k=kb):
                    slot = k % R
                    wait_unit(ag_recv.at[slot, zp])
                    there = block(k, zp, c)

                    @pl.when(z < 3)
                    def _():
                        remote(there, there, ag_send.at[slot, zp], ag_recv.at[slot, zp], up).start()

                    remote(there, there, p_send.at[slot, zp], p_recv.at[slot, zp], partner).start()

                zq = 1 + near
                kc = t - F_OF[zq] - (zq - z) * G

                @pl.when(live(kc) & (zq > z))
                def _(zq=zq, k=kc):
                    slot = k % R
                    wait_unit(ag_recv.at[slot, zq])
                    there = block(k, zq, c)

                    @pl.when(z > 0)
                    def _():
                        remote(there, there, ag_send.at[slot, zq], ag_recv.at[slot, zq], down).start()

                    remote(there, there, p_send.at[slot, zq], p_recv.at[slot, zq], partner).start()

        for i in ORDER:
            (sums, take_step, spread)[i]()

        for zp in range(4):
            ksent = t - F_OF[zp] - jnp.abs(z - zp) * G

            @pl.when(live(ksent - 1))
            def _(zp=zp, k=ksent - 1):
                wait_unit(p_recv.at[k % R, zp])

            @pl.when(live(ksent - LATE))
            def _(zp=zp, k=ksent - LATE):
                wait_unit(p_send.at[k % R, zp])

                @pl.when((zp < z) & (z < 3))
                def _():
                    wait_unit(ag_send.at[k % R, zp])

                @pl.when((zp > z) & (z > 0))
                def _():
                    wait_unit(ag_send.at[k % R, zp])

                @pl.when((zp == z) & (z < 3))
                def _():
                    wait_unit(ag_send.at[k % R, zp])

                @pl.when((zp == z) & (z > 0))
                def _():
                    wait_unit(ag_send.at[k % R, 4])

        return 0

    lax.fori_loop(0, STEPS, body, 0)


def put_out(*refs):
    W, MVV, MV = refs[0:3]
    whole, rest = refs[3:6], refs[6:12]
    held, load, store, keep = refs[12:16]
    parts = [(which, i, layer) for i in range(NV, 3) for which in range(2) for layer in range(2)]
    for j, (which, i, layer) in enumerate(parts):
        pltpu.make_async_copy(MV.at[which, i - NV, layer], held.at[j], load.at[j]).start()
    copies = [pltpu.make_async_copy(W.at[i, l], whole[i].at[l], keep.at[7 + 2 * i + l]) for i in range(3) for l in range(2)]
    for i in range(NV):
        for which in range(2):
            copies.append(pltpu.make_async_copy(MVV.at[which, i], rest[3 * which + i].at[:, 0], keep.at[3 + 2 * i + which]))
    for copy in copies:
        copy.start()
    for j, (which, i, layer) in enumerate(parts):
        pltpu.make_async_copy(MV.at[which, i - NV, layer], held.at[j], load.at[j]).wait()
        copy = pltpu.make_async_copy(held.at[j], rest[3 * which + i].at[layer, 0], store.at[j])
        copy.start()
        copies.append(copy)
    for copy in copies:
        copy.wait()


def solution(mesh):
    def step(*arrays):
        g = [tiled(a[0], 8).reshape(2, 4, 2, UNITS, 16, 128) for a in arrays[:3]]
        w = [tiled(a, 8) for a in arrays[3:6]]
        moments = [tiled(a, 1) for a in arrays[6:]]
        hbm, vmem = pl.BlockSpec(memory_space=pl.ANY), pl.BlockSpec(memory_space=pltpu.VMEM)
        piece = (N, 16, 128)
        dma = pltpu.SemaphoreType.DMA
        new, kept, mv = pl.pallas_call(
            kernel,
            out_shape=[
                pltpu.VMEM((3, 2, 8, UNITS, 16, 128), jnp.bfloat16),
                pltpu.VMEM((2, NV, 2, UNITS, 16, 128), jnp.float32),
                jax.ShapeDtypeStruct((2, 3 - NV, 2, UNITS, 16, 128), jnp.float32),
            ],
            in_specs=[hbm] * 12,
            out_specs=[vmem, vmem, hbm],
            scratch_shapes=[
                pltpu.VMEM((R, 4, *piece), jnp.bfloat16),
                pltpu.VMEM((R, 4, *piece), jnp.bfloat16),
                pltpu.VMEM((R, 5, *piece), jnp.bfloat16),
                pltpu.VMEM((R2, 2, *piece), jnp.float32),
                dma((R,)),
                dma((R,)),
                dma((R,)),
                dma((R, 4)),
                dma((R, 5)),
                dma((R2, 3)),
                dma((R2, 2)),
                dma((R, 5)),
                dma((R, 4)),
                dma((R, 4)),
                dma((R, 4)),
            ],
            compiler_params=pltpu.CompilerParams(collective_id=0, has_side_effects=True, vmem_limit_bytes=int(LIMIT * 2**20)),
            name="sum_step_spread",
        )(*g, *w, *moments)
        parts = 4 * (3 - NV)
        outs = pl.pallas_call(
            put_out,
            out_shape=[jax.ShapeDtypeStruct((2, 8, UNITS, 16, 128), jnp.bfloat16)] * 3 + [jax.ShapeDtypeStruct((2, 1, UNITS, 16, 128), jnp.float32)] * 6,
            in_specs=[vmem, vmem, hbm],
            out_specs=[hbm] * 9,
            scratch_shapes=[pltpu.VMEM((parts, UNITS, 16, 128), jnp.float32), dma((parts,)), dma((parts,)), dma((13,))],
            compiler_params=pltpu.CompilerParams(vmem_limit_bytes=int(LIMIT * 2**20)),
            name="put_out",
        )(*(pltpu.with_memory_space_constraint(x, pltpu.VMEM) for x in (new, kept)), pltpu.with_memory_space_constraint(mv, pltpu.HBM))
        whole = [untiled(outs[i], *SHAPES[i]) for i in range(3)]
        rest = [untiled(outs[3 + i], SHAPES[i % 3][0] // 8, SHAPES[i % 3][1]) for i in range(6)]
        return (*whole, *rest)

    all_of, cut = P(None, None, None), P(None, "dp", None)
    return jax.shard_map(
        step,
        mesh=mesh,
        in_specs=(P(("rep", "dp"), None, None, None),) * 3 + (all_of,) * 3 + (cut,) * 6,
        out_specs=(P("rep", None, None),) * 3 + (P("rep", "dp", None),) * 6,
        check_vma=False,
    )
```

time: 518 us -> 517 us (level)
  no operation moved by 1% of the time
where the time goes in v3:
time: 517 us
  Pallas kernels  516 us (100%)
    pallas_call x1, Pallas kernels, step(): pl.pallas_call(kernel, out_shape=[pltpu.VMEM((3, 2, 8, UNITS, 16, 128), j...  493 us
    pallas_call x1, Pallas kernels, step(): pl.pallas_call(put_out, out_shape=[jax.ShapeDtypeStruct((2, 8, UNITS, 16,...  22.9 us

profile of v3, /device:TPU:0, one launch (start us, length us, event | category | flops | bytes accessed | tf_op | source)
XLA Modules:
  0.0 516.8 jit_solution(3912615708756067630)
XLA Ops:
  0.6 493.2 %sum_step_spread.1 = (bf16[3,2,8,224,16,128]{5,4,3,2,1,0:T(8,128)(2,1)S(1)}, f32[2,2,2,224,16,128]{5,4,3,2,1,0:T(8,128)S(1)}, f32[2,1,2,224,16,128]{5,4,3,2,1,0:T(8,128)}) custom-call(bf16[2,4,2,224,16,128]{5,4,3,2,1,0:T(8,128)(2,1)} %bitcast.105, bf16[2,4,2,224,16,128]{5,4,3,2,1,0:T(8,128)(2,1)} %bitcast.106, bf16[2,4,2,224,16,128]{5,4,3,2,1,0:T(8,128)(2,1)} %bitcast.107, ...), custom_call_target="tpu_custom_call" | custom-call | tf_op jit(solution)/shard_map/sum_step_spread/pallas_call | solution.py:378
  493.9 22.9 %put_out.1 = (bf16[2,8,224,16,128]{4,3,2,1,0:T(8,128)(2,1)}, bf16[2,8,224,16,128]{4,3,2,1,0:T(8,128)(2,1)}, bf16[2,8,224,16,128]{4,3,2,1,0:T(8,128)(2,1)}, f32[2...) custom-call(bf16[3,2,8,224,16,128]{5,4,3,2,1,0:T(8,128)(2,1)S(1)} %g, ...), custom_call_target="tpu_custom_call" | custom-call | tf_op jit(solution)/shard_map/put_out/pallas_call | solution.py:408

commit v4 on v3

--- a/solution.py
+++ b/solution.py
@@ -14,6 +14,7 @@
 K = 6 * PER
 H = 1
 AHEAD = 1
+FIRST = 4
 EARLY = 2
 LATE = 3
 R = 8
@@ -21,7 +22,7 @@
 S = 2
 G = 1
 ORDER = (0, 1, 2)
-CH = 7
+CH = 14
 NV = 2
 LIMIT = 7.75
 SHAPES = ((1024, 3584), (1024, 3584), (3584, 1024))
@@ -108,12 +109,12 @@
     def _():
         pl.semaphore_signal(barrier, inc=1, device_id={"dp": down}, device_id_type=MESH)
 
-    for k in range(AHEAD):
+    for k in range(FIRST):
         load_own(k)
 
     pl.semaphore_wait(barrier, jnp.where((z == 0) | (z == 3), 2, 3))
 
-    for k in range(AHEAD):
+    for k in range(FIRST):
         send_part(k)
 
     def add(slot, zp, more):
@@ -168,7 +169,7 @@
 
         ka = t + AHEAD
 
-        @pl.when(live(ka))
+        @pl.when(live(ka) & (ka >= FIRST))
         def _():
             load_own(ka)
             send_part(ka)

time: 517 us -> 517 us (level)
  no operation moved by 1% of the time
where the time goes in v4:
time: 517 us
  Pallas kernels  516 us (100%)
    pallas_call x1, Pallas kernels, step(): pl.pallas_call(kernel, out_shape=[pltpu.VMEM((3, 2, 8, UNITS, 16, 128), j...  493 us
    pallas_call x1, Pallas kernels, step(): pl.pallas_call(put_out, out_shape=[jax.ShapeDtypeStruct((2, 8, UNITS, 16,...  22.9 us

profile of v4, /device:TPU:0, one launch (start us, length us, event | category | flops | bytes accessed | tf_op | source)
XLA Modules:
  0.0 516.7 jit_solution(7058115401503232479)
XLA Ops:
  0.6 493.1 %sum_step_spread.1 = (bf16[3,2,8,224,16,128]{5,4,3,2,1,0:T(8,128)(2,1)S(1)}, f32[2,2,2,224,16,128]{5,4,3,2,1,0:T(8,128)S(1)}, f32[2,1,2,224,16,128]{5,4,3,2,1,0:T(8,128)}) custom-call(bf16[2,4,2,224,16,128]{5,4,3,2,1,0:T(8,128)(2,1)} %bitcast.105, bf16[2,4,2,224,16,128]{5,4,3,2,1,0:T(8,128)(2,1)} %bitcast.106, bf16[2,4,2,224,16,128]{5,4,3,2,1,0:T(8,128)(2,1)} %bitcast.107, ...), custom_call_target="tpu_custom_call" | custom-call | tf_op jit(solution)/shard_map/sum_step_spread/pallas_call | solution.py:379
  493.8 22.9 %put_out.1 = (bf16[2,8,224,16,128]{4,3,2,1,0:T(8,128)(2,1)}, bf16[2,8,224,16,128]{4,3,2,1,0:T(8,128)(2,1)}, bf16[2,8,224,16,128]{4,3,2,1,0:T(8,128)(2,1)}, f32[2...) custom-call(bf16[3,2,8,224,16,128]{5,4,3,2,1,0:T(8,128)(2,1)S(1)} %g, ...), custom_call_target="tpu_custom_call" | custom-call | tf_op jit(solution)/shard_map/put_out/pallas_call | solution.py:409
